TPU v7x, 256 devices: a whole 4x4x8 slice. The times are simulated.
256 devices in a mesh: cp: 64 (over z_hi, y, x, core), tp: 4 (over z_lo).
Axes of the slice: x: 4, y: 4, z: 8 (z_hi: 2, z_lo: 4; z = z_hi * 4 + z_lo), core: 2. Of those that a mesh axis runs over, the one named last changes fastest.
Arguments:
- queries: bfloat16 [49152, 5120], P('cp', 'tp'), may hold values from -36 to 36
- keys: bfloat16 [49152, 1024], P('cp', 'tp'), may hold values from -5 to 5
- values: bfloat16 [49152, 1024], P('cp', 'tp'), may hold values from -6 to 6
- doc_lengths: int32 [64], replicated, may hold values from 1 to 1536, 49152 in all
Outputs:
- attended: bfloat16 [49152, 5120], P(('cp', 'tp'))
Inputs may be any that keep to these rules, and one draw needn't show every extreme that they name: `doc_lengths`: they sum to 49152, and one of them is exactly 1536.
All inputs are finite; a program needn't handle non-finite values.
Results may differ from a plain program's by a relative error of at most 0.0038.
Values may be sent and summed in bfloat16 or wider, within the bound.
A program may use at most 256 MiB of HBM per device.

v0:
```python
import jax
import jax.numpy as jnp
from jax import lax
from jax.sharding import PartitionSpec as P

HEAD = 128
DOC_DEVS = 2


negative = -1e30


def from_behind(block, axis, distance):
    devices = range(lax.axis_size(axis))
    route = [(i - distance, i) for i in devices if i - distance in devices]
    return lax.ppermute(block, axis, route)


def doc_index(positions, doc_ends):
    return jnp.sum((positions[..., None] >= doc_ends).astype(jnp.int32), axis=-1)


def on_device(queries, keys, values, doc_lengths):
    tok_rows, q_cols = queries.shape
    kv_cols = keys.shape[1]
    kv_local = kv_cols // HEAD
    group_size = q_cols // kv_cols
    half_rows = tok_rows // 2
    cp_size = lax.axis_size("cp")
    my_index = lax.axis_index("cp")
    stretch_span = 2 * min(DOC_DEVS, cp_size // 2)
    dev_reach = min(stretch_span, cp_size - 1)
    doc_ends = jnp.cumsum(doc_lengths)
    paired = jnp.stack([keys, values])
    from_below = paired[:, :half_rows]
    from_above = paired
    below_list = []
    above_list = []
    for turn_number in range(dev_reach):
        from_below = from_behind(from_below, "cp", 1)
        from_above = from_behind(from_above, "cp", -1)
        below_list.append(jnp.concatenate([from_below, jnp.zeros_like(from_below)], axis=1))
        above_list.append(from_above)
    kv_bank = jnp.stack(below_list[::-1] + [paired] + above_list)
    slot_offset = dev_reach - my_index
    bank_slots = kv_bank.shape[0]
    kv_bank = kv_bank.reshape(bank_slots, 2, 2, half_rows, kv_local, HEAD)
    stretch_ids = jnp.stack([my_index, 2 * cp_size - 1 - my_index])
    offsets = jnp.arange(half_rows, dtype=jnp.int32)
    q_pos = stretch_ids[:, None] * half_rows + offsets[None, :]
    q_doc = doc_index(q_pos, doc_ends)
    q_blocks = queries.reshape(2, half_rows, kv_local, group_size, HEAD)
    scale = float(HEAD) ** (-0.5)

    def fetch_block(kv_slot, kv_part):
        kv_piece = lax.dynamic_index_in_dim(kv_bank, kv_slot, 0, keepdims=False)
        return lax.dynamic_index_in_dim(kv_piece, kv_part, 1, keepdims=False)

    def one_tile(tile_step, state_now):
        needed = stretch_ids - tile_step
        present = needed >= 0
        clamped = jnp.maximum(needed, 0)
        device_ids = jnp.where(clamped < cp_size, clamped, 2 * cp_size - 1 - clamped)
        kv_part = (clamped >= cp_size).astype(jnp.int32)
        kv_slot = jnp.clip(device_ids + slot_offset, 0, bank_slots - 1)
        k_pos = clamped[:, None] * half_rows + offsets[None, :]
        k_doc = doc_index(k_pos, doc_ends)
        allowed = (
            present[:, None, None]
            & (k_doc[:, None, :] == q_doc[:, :, None])
            & (k_pos[:, None, :] <= q_pos[:, :, None])
        )

        def update(state_old):
            running_max, running_sum, running_out = state_old
            pieces = jnp.stack([fetch_block(kv_slot[which], kv_part[which]) for which in range(2)])
            scores = (
                jnp.einsum(
                    "cqhjd,ckhd->cqhjk", q_blocks, pieces[:, 0], preferred_element_type=jnp.float32
                )
                * scale
            )
            allowed_wide = allowed[:, :, None, None, :]
            scores = jnp.where(allowed_wide, scores, negative)
            new_max = jnp.maximum(running_max, jnp.max(scores, axis=-1))
            weights = jnp.where(allowed_wide, jnp.exp(scores - new_max[..., None]), 0.0)
            rescale = jnp.exp(running_max - new_max)
            new_sum = rescale * running_sum + jnp.sum(weights, axis=-1)
            product = jnp.einsum(
                "cqhjk,ckhd->cqhjd",
                weights.astype(jnp.bfloat16),
                pieces[:, 1],
                preferred_element_type=jnp.float32,
            )
            new_out = rescale[..., None] * running_out + product
            return (new_max, new_sum, new_out)

        return lax.cond(jnp.any(allowed), update, lambda state_old: state_old, state_now)

    start_state = (
        jnp.full((2, half_rows, kv_local, group_size), negative, jnp.float32),
        jnp.zeros((2, half_rows, kv_local, group_size), jnp.float32),
        jnp.zeros((2, half_rows, kv_local, group_size, HEAD), jnp.float32),
    )
    final_max, final_sum, final_out = lax.fori_loop(0, stretch_span + 1, one_tile, start_state)
    attended = (final_out / final_sum[..., None]).reshape(tok_rows, q_cols).astype(jnp.bfloat16)
    return lax.all_to_all(attended, "tp", split_axis=0, concat_axis=1, tiled=True)


def solution(mesh):
    in_specs = (P("cp", "tp"), P("cp", "tp"), P("cp", "tp"), P())
    out_specs = P(("cp", "tp"), None)
    return jax.shard_map(
        on_device, mesh=mesh, in_specs=in_specs, out_specs=out_specs, check_vma=False
    )
```

profile of v0, /device:TPU:128, one launch (start us, length us, event | category | flops | bytes accessed | tf_op | source)
XLA Modules:
  0.0 306.7 jit_solution(16265387829623437843)
XLA Ops:
  0.0 1.2 pad_maximum_fusion.1
  1.2 4.7 %collective-permute-start.4 = (bf16[2,768,256]{2,1,0:T(8,128)(2,1)S(1)}, bf16[2,768,256]{2,1,0:T(8,128)(2,1)S(1)}, u32[]{:S(2)}, u32[]{:S(2)}) collective-permute-start(bf16[2,768,256]{2,1,0:T(8,128)(2,1)S(1)} %pad_maximum_fusion.1), channel_id=1, source_target_pairs={{4,0},{8,4},{12,8},{16,12},{20,16},{24,20},{28,24},{32,28},{36,32}... | collective-permute-start | bytes 2359304 | tf_op jit(solution)/shard_map/ppermute | solution.py:16
  7.0 1.9 collective-permute-start
  8.9 6.5 %collective-permute-done.4 = bf16[2,768,256]{2,1,0:T(8,128)(2,1)S(1)} collective-permute-done((bf16[2,768,256]{2,1,0:T(8,128)(2,1)S(1)}, bf16[2,768,256]{2,1,0:T(8,128)(2,1)S(1)}, u32[]{:S(2)}, u32[]{:S(2)}) %collective-permute-start.4) | collective-permute-done | bytes 786464 | tf_op jit(solution)/shard_map/ppermute | solution.py:16
  16.3 12.0 %collective-permute-start.5 = (bf16[2,768,256]{2,1,0:T(8,128)(2,1)S(1)}, bf16[2,768,256]{2,1,0:T(8,128)(2,1)}, u32[]{:S(2)}, u32[]{:S(2)}) collective-permute-start(bf16[2,768,256]{2,1,0:T(8,128)(2,1)S(1)} %collective-permute-done.4), channel_id=1, source_target_pairs={{4,0},{8,4},{12,8},{16,12},{20,16},{24,20},{28,24},{32,28},{36,32}... | collective-permute-start | bytes 2359304 | tf_op jit(solution)/shard_map/ppermute | solution.py:16
  28.4 1.9 collective-permute-start.1
  30.3 15.3 %collective-permute-done.1 = bf16[2,384,256]{2,1,0:T(8,128)(2,1)S(1)} collective-permute-done((bf16[2,384,256]{2,1,0:T(8,128)(2,1)S(1)}, bf16[2,384,256]{2,1,0:T(8,128)(2,1)S(1)}, u32[]{:S(2)}, u32[]{:S(2)}) %collective-permute-start.1) | collective-permute-done | bytes 393248 | tf_op jit(solution)/shard_map/ppermute | solution.py:16
  45.6 1.9 collective-permute-start.2
  47.5 11.8 %collective-permute-start.6 = (bf16[2,768,256]{2,1,0:T(8,128)(2,1)}, bf16[2,768,256]{2,1,0:T(8,128)(2,1)}, u32[]{:S(2)}, u32[]{:S(2)}) collective-permute-start(bf16[2,768,256]{2,1,0:T(8,128)(2,1)} %collective-permute-done.5), channel_id=1, source_target_pairs={{4,0},{8,4},{12,8},{16,12},{20,16},{24,20},{28,24},{32,28},{36,32}... | collective-permute-start | bytes 2359304 | tf_op jit(solution)/shard_map/ppermute | solution.py:16
  59.3 3.6 %collective-permute-done.2 = bf16[2,384,256]{2,1,0:T(8,128)(2,1)} collective-permute-done((bf16[2,384,256]{2,1,0:T(8,128)(2,1)S(1)}, bf16[2,384,256]{2,1,0:T(8,128)(2,1)}, u32[]{:S(2)}, u32[]{:S(2)}) %collective-permute-start.2) | collective-permute-done | bytes 393248 | tf_op jit(solution)/shard_map/ppermute | solution.py:16
  62.9 1.9 collective-permute-start.3
  64.9 1.8 stack.74
  66.7 1.9 stack.75
  69.5 5.6 %reshape.177 = bf16[2,384,2,5,128]{4,3,2,1,0:T(8,128)(2,1)} reshape(bf16[768,1280]{1,0:T(8,128)(2,1)} %param.8) | data formatting | bytes 3932160 | tf_op jit(solution)/shard_map/reshape | solution.py:52
  75.2 2.4 copy.37
  80.2 2.0 stack.77
  82.2 1.9 concatenate.19
  84.1 2.7 stack.71
  86.8 1.9 concatenate.18
  88.8 2.7 stack.70
  91.5 2.7 stack.78
  94.2 2.6 constant_dynamic-update-slice_fusion.7
  96.8 2.6 constant_dynamic-update-slice_fusion.6
  99.5 11.8 %collective-permute-start.7 = (bf16[2,768,256]{2,1,0:T(8,128)(2,1)}, bf16[2,768,256]{2,1,0:T(8,128)(2,1)}, u32[]{:S(2)}, u32[]{:S(2)}) collective-permute-start(bf16[2,768,256]{2,1,0:T(8,128)(2,1)} %collective-permute-done.6), channel_id=1, source_target_pairs={{4,0},{8,4},{12,8},{16,12},{20,16},{24,20},{28,24},{32,28},{36,32}... | collective-permute-start | bytes 2359304 | tf_op jit(solution)/shard_map/ppermute | solution.py:16
  111.2 2.6 constant_dynamic-update-slice_fusion.5
  113.9 1.4 constant_dynamic-update-slice_fusion.4
  115.3 2.7 maximum_dynamic-update-slice_fusion
  118.0 1.4 constant_dynamic-update-slice_fusion.3
  119.4 1.4 constant_dynamic-update-slice_fusion.2
  120.8 2.0 stack.79
  122.9 1.5 constant_dynamic-update-slice_fusion.1
  124.3 2.0 stack.80
  126.3 1.4 constant_dynamic-update-slice_fusion
  127.8 7.7 %copy.36 = bf16[9,2,2,384,2,128]{5,3,4,1,2,0:T(8,128)(2,1)} copy(bf16[9,2,2,384,2,128]{5,4,3,2,1,0:T(2,128)(2,1)} %constant_dynamic-update-slice_fusion) | data formatting | bytes 14155776
  135.5 2.4 broadcast_in_dim.67
  137.9 118.7 %while.18 = (s32[]{:T(128)}, f32[2,384,2,5]{1,3,2,0:T(8,128)S(1)}, f32[2,384,2,5]{1,3,2,0:T(8,128)S(1)}, f32[2,384,2,5,128]{1,4,3,2,0:T(8,128)}, s32[2]{0:T(128)...) while((s32[]{:T(128)}, f32[2,384,2,5]{1,3,2,0:T(8,128)S(1)}, ...), condition=%wide.region_9.10_spmd.clone, body=%wide.region_2.9_spmd.clone.sunk | while | flops 1553465088 | bytes 50062192 | solution.py:105
  139.8 21.8 %conditional.3 = ((f32[2,384,2,5]{1,3,2,0:T(8,128)S(1)}, f32[2,384,2,5]{1,3,2,0:T(8,128)S(1)}, f32[2,384,2,5,128]{1,4,3,2,0:T(8,128)})) conditional(s32[]{:T(128)} %convert_element_type.54, (f32[2,384,2,5]{1,3,2,0:T(8,128)S(1)}, f32[2,384,2,5]{1,3,2,0:T(8,128)S(1)}, f32[2,384,2,5,128]{1,4,3,2,0:T(8,128)}) %tuple.70, ...), branch_computations={%region_5.5_spmd, %region_6.8_spmd} | conditional | flops 1551842304 | bytes 49742132 | solution.py:98
  148.7 1.2 dynamic-slice_bitcast_fusion
  149.9 2.0 fusion.4
  152.0 2.9 fusion.6
  154.9 6.8 %bitcast_add_fusion = f32[2,384,2,5,128]{1,4,3,2,0:T(8,128)} fusion(f32[2,384,2,5,128]{1,4,3,2,0:T(8,128)} %get-tuple-element.270, f32[2,2,384,384,5]{3,2,4,1,0:T(8,128)S(1)} %get-tuple-element.401, f32[2,384,2,5]{1,3,2,0:T(8,128)S(1)} %max.21, pred[2,384,384]{1,2,0:T(8,128)(4,1)S(1)} %get-tuple-element.262, f32[2,384,2,5]{1,3,2,0:T(8,128)S(1)} %get-tuple-element.387, ...), kind=kOutput, calls=%fused_computation.9 | convolution fusion | flops 772472832 | bytes 20803584 | tf_op jit(solution)/shard_map/while/body/eval_jaxpr/cond/branch_1_fun/cqhjk,ckhd->cqhjd/dot_general | solution.py:89
  163.6 21.8 %conditional.3 = ((f32[2,384,2,5]{1,3,2,0:T(8,128)S(1)}, f32[2,384,2,5]{1,3,2,0:T(8,128)S(1)}, f32[2,384,2,5,128]{1,4,3,2,0:T(8,128)})) conditional(s32[]{:T(128)} %convert_element_type.54, (f32[2,384,2,5]{1,3,2,0:T(8,128)S(1)}, f32[2,384,2,5]{1,3,2,0:T(8,128)S(1)}, f32[2,384,2,5,128]{1,4,3,2,0:T(8,128)}) %tuple.70, ...), branch_computations={%region_5.5_spmd, %region_6.8_spmd} | conditional | flops 1551842304 | bytes 49742132 | solution.py:98
  173.6 2.0 fusion.4
  175.7 2.9 fusion.6
  178.6 6.8 %bitcast_add_fusion = f32[2,384,2,5,128]{1,4,3,2,0:T(8,128)} fusion(f32[2,384,2,5,128]{1,4,3,2,0:T(8,128)} %get-tuple-element.270, f32[2,2,384,384,5]{3,2,4,1,0:T(8,128)S(1)} %get-tuple-element.401, f32[2,384,2,5]{1,3,2,0:T(8,128)S(1)} %max.21, pred[2,384,384]{1,2,0:T(8,128)(4,1)S(1)} %get-tuple-element.262, f32[2,384,2,5]{1,3,2,0:T(8,128)S(1)} %get-tuple-element.387, ...), kind=kOutput, calls=%fused_computation.9 | convolution fusion | flops 772472832 | bytes 20803584 | tf_op jit(solution)/shard_map/while/body/eval_jaxpr/cond/branch_1_fun/cqhjk,ckhd->cqhjd/dot_general | solution.py:89
  187.3 21.8 %conditional.3 = ((f32[2,384,2,5]{1,3,2,0:T(8,128)S(1)}, f32[2,384,2,5]{1,3,2,0:T(8,128)S(1)}, f32[2,384,2,5,128]{1,4,3,2,0:T(8,128)})) conditional(s32[]{:T(128)} %convert_element_type.54, (f32[2,384,2,5]{1,3,2,0:T(8,128)S(1)}, f32[2,384,2,5]{1,3,2,0:T(8,128)S(1)}, f32[2,384,2,5,128]{1,4,3,2,0:T(8,128)}) %tuple.70, ...), branch_computations={%region_5.5_spmd, %region_6.8_spmd} | conditional | flops 1551842304 | bytes 49742132 | solution.py:98
  196.2 1.2 dynamic-slice_bitcast_fusion
  197.4 2.0 fusion.4
  199.4 2.9 fusion.6
  202.4 6.8 %bitcast_add_fusion = f32[2,384,2,5,128]{1,4,3,2,0:T(8,128)} fusion(f32[2,384,2,5,128]{1,4,3,2,0:T(8,128)} %get-tuple-element.270, f32[2,2,384,384,5]{3,2,4,1,0:T(8,128)S(1)} %get-tuple-element.401, f32[2,384,2,5]{1,3,2,0:T(8,128)S(1)} %max.21, pred[2,384,384]{1,2,0:T(8,128)(4,1)S(1)} %get-tuple-element.262, f32[2,384,2,5]{1,3,2,0:T(8,128)S(1)} %get-tuple-element.387, ...), kind=kOutput, calls=%fused_computation.9 | convolution fusion | flops 772472832 | bytes 20803584 | tf_op jit(solution)/shard_map/while/body/eval_jaxpr/cond/branch_1_fun/cqhjk,ckhd->cqhjd/dot_general | solution.py:89
  211.0 21.8 %conditional.3 = ((f32[2,384,2,5]{1,3,2,0:T(8,128)S(1)}, f32[2,384,2,5]{1,3,2,0:T(8,128)S(1)}, f32[2,384,2,5,128]{1,4,3,2,0:T(8,128)})) conditional(s32[]{:T(128)} %convert_element_type.54, (f32[2,384,2,5]{1,3,2,0:T(8,128)S(1)}, f32[2,384,2,5]{1,3,2,0:T(8,128)S(1)}, f32[2,384,2,5,128]{1,4,3,2,0:T(8,128)}) %tuple.70, ...), branch_computations={%region_5.5_spmd, %region_6.8_spmd} | conditional | flops 1551842304 | bytes 49742132 | solution.py:98
  221.1 2.0 fusion.4
  223.2 2.9 fusion.6
  226.1 6.8 %bitcast_add_fusion = f32[2,384,2,5,128]{1,4,3,2,0:T(8,128)} fusion(f32[2,384,2,5,128]{1,4,3,2,0:T(8,128)} %get-tuple-element.270, f32[2,2,384,384,5]{3,2,4,1,0:T(8,128)S(1)} %get-tuple-element.401, f32[2,384,2,5]{1,3,2,0:T(8,128)S(1)} %max.21, pred[2,384,384]{1,2,0:T(8,128)(4,1)S(1)} %get-tuple-element.262, f32[2,384,2,5]{1,3,2,0:T(8,128)S(1)} %get-tuple-element.387, ...), kind=kOutput, calls=%fused_computation.9 | convolution fusion | flops 772472832 | bytes 20803584 | tf_op jit(solution)/shard_map/while/body/eval_jaxpr/cond/branch_1_fun/cqhjk,ckhd->cqhjd/dot_general | solution.py:89
  234.8 21.8 %conditional.3 = ((f32[2,384,2,5]{1,3,2,0:T(8,128)S(1)}, f32[2,384,2,5]{1,3,2,0:T(8,128)S(1)}, f32[2,384,2,5,128]{1,4,3,2,0:T(8,128)})) conditional(s32[]{:T(128)} %convert_element_type.54, (f32[2,384,2,5]{1,3,2,0:T(8,128)S(1)}, f32[2,384,2,5]{1,3,2,0:T(8,128)S(1)}, f32[2,384,2,5,128]{1,4,3,2,0:T(8,128)}) %tuple.70, ...), branch_computations={%region_5.5_spmd, %region_6.8_spmd} | conditional | flops 1551842304 | bytes 49742132 | solution.py:98
  243.7 1.2 dynamic-slice_bitcast_fusion
  244.9 2.0 fusion.4
  246.9 2.9 fusion.6
  249.8 6.8 %bitcast_add_fusion = f32[2,384,2,5,128]{1,4,3,2,0:T(8,128)} fusion(f32[2,384,2,5,128]{1,4,3,2,0:T(8,128)} %get-tuple-element.270, f32[2,2,384,384,5]{3,2,4,1,0:T(8,128)S(1)} %get-tuple-element.401, f32[2,384,2,5]{1,3,2,0:T(8,128)S(1)} %max.21, pred[2,384,384]{1,2,0:T(8,128)(4,1)S(1)} %get-tuple-element.262, f32[2,384,2,5]{1,3,2,0:T(8,128)S(1)} %get-tuple-element.387, ...), kind=kOutput, calls=%fused_computation.9 | convolution fusion | flops 772472832 | bytes 20803584 | tf_op jit(solution)/shard_map/while/body/eval_jaxpr/cond/branch_1_fun/cqhjk,ckhd->cqhjd/dot_general | solution.py:89
  256.6 3.8 %divide_convert_fusion = bf16[2,384,2,5,128]{1,4,3,2,0:T(8,128)(2,1)} fusion(f32[2,384,2,5,128]{1,4,3,2,0:T(8,128)} %get-tuple-element.289, f32[2,384,2,5]{1,3,2,0:T(8,128)S(1)} %get-tuple-element.290), kind=kLoop, calls=%fused_computation.37 | loop fusion | flops 1966080 | bytes 5928960 | tf_op jit(solution)/shard_map/convert_element_type | solution.py:106
  260.4 3.8 %copy.48 = bf16[2,384,2,5,128]{4,3,2,1,0:T(8,128)(2,1)S(1)} copy(bf16[2,384,2,5,128]{1,4,3,2,0:T(8,128)(2,1)} %divide_convert_fusion) | data formatting | bytes 3932160 | tf_op jit(solution)/shard_map/convert_element_type | solution.py:106
  264.3 3.2 %reshape.178 = bf16[4,192,1280]{2,1,0:T(8,128)(2,1)} reshape(bf16[2,384,2,5,128]{4,3,2,1,0:T(8,128)(2,1)S(1)} %copy.48) | data formatting | bytes 3932160 | tf_op jit(solution)/shard_map/convert_element_type | solution.py:106
  267.5 37.7 %all_to_all.16 = bf16[4,192,1280]{2,1,0:T(8,128)(2,1)S(1)} all-to-all(bf16[4,192,1280]{2,1,0:T(8,128)(2,1)} %reshape.178), channel_id=1, replica_groups=mesh['cp'=64,'tp'=4] {'tp'}, dimensions={0} | all-to-all | bytes 3932160 | tf_op jit(solution)/shard_map/all_to_all | solution.py:107
  305.2 1.5 copy.50
  (86 shorter events, 20.2 us)
Async XLA Ops:
  1.2 14.2 %collective-permute-start.4 = (bf16[2,768,256]{2,1,0:T(8,128)(2,1)S(1)}, bf16[2,768,256]{2,1,0:T(8,128)(2,1)S(1)}, u32[]{:S(2)}, u32[]{:S(2)}) collective-permute-start(bf16[2,768,256]{2,1,0:T(8,128)(2,1)S(1)} %pad_maximum_fusion.1), channel_id=1, source_target_pairs={{4,0},{8,4},{12,8},{16,12},{20,16},{24,20},{28,24},{32,28},{36,32}... | collective-permute-start | bytes 2359304 | tf_op jit(solution)/shard_map/ppermute | solution.py:16
  7.0 21.3 %collective-permute-start = (bf16[2,384,256]{2,1,0:T(8,128)(2,1)S(1)}, bf16[2,384,256]{2,1,0:T(8,128)(2,1)S(1)}, u32[]{:S(2)}, u32[]{:S(2)}) collective-permute-start(bf16[2,384,256]{2,1,0:T(8,128)(2,1)S(1)} %fusion.24), channel_id=1, source_target_pairs={{0,4},{4,8},{8,12},{12,16},{16,20},{20,24},{24,28},{28,32},{32,36}... | collective-permute-start | bytes 1179656 | tf_op jit(solution)/shard_map/ppermute | solution.py:16
  15.4 0.9 copy-start.1
  16.3 31.2 %collective-permute-start.5 = (bf16[2,768,256]{2,1,0:T(8,128)(2,1)S(1)}, bf16[2,768,256]{2,1,0:T(8,128)(2,1)}, u32[]{:S(2)}, u32[]{:S(2)}) collective-permute-start(bf16[2,768,256]{2,1,0:T(8,128)(2,1)S(1)} %collective-permute-done.4), channel_id=1, source_target_pairs={{4,0},{8,4},{12,8},{16,12},{20,16},{24,20},{28,24},{32,28},{36,32}... | collective-permute-start | bytes 2359304 | tf_op jit(solution)/shard_map/ppermute | solution.py:16
  28.4 17.2 %collective-permute-start.1 = (bf16[2,384,256]{2,1,0:T(8,128)(2,1)S(1)}, bf16[2,384,256]{2,1,0:T(8,128)(2,1)S(1)}, u32[]{:S(2)}, u32[]{:S(2)}) collective-permute-start(bf16[2,384,256]{2,1,0:T(8,128)(2,1)S(1)} %collective-permute-done), channel_id=1, source_target_pairs={{0,4},{4,8},{8,12},{12,16},{16,20},{20,24},{24,28},{28,32},{32,36}... | collective-permute-start | bytes 1179656 | tf_op jit(solution)/shard_map/ppermute | solution.py:16
  45.6 24.0 %copy-start.2 = (bf16[2,384,256]{2,1,0:T(8,128)(2,1)}, bf16[2,384,256]{2,1,0:T(8,128)(2,1)S(1)}, u32[]{:S(2)}) copy-start(bf16[2,384,256]{2,1,0:T(8,128)(2,1)S(1)} %collective-permute-done.1) | copy-start | bytes 1179652
  45.6 17.3 %collective-permute-start.2 = (bf16[2,384,256]{2,1,0:T(8,128)(2,1)S(1)}, bf16[2,384,256]{2,1,0:T(8,128)(2,1)}, u32[]{:S(2)}, u32[]{:S(2)}) collective-permute-start(bf16[2,384,256]{2,1,0:T(8,128)(2,1)S(1)} %collective-permute-done.1), channel_id=1, source_target_pairs={{0,4},{4,8},{8,12},{12,16},{16,20},{20,24},{24,28},{28,32},{32,36}... | collective-permute-start | bytes 1179656 | tf_op jit(solution)/shard_map/ppermute | solution.py:16
  47.5 52.0 %collective-permute-start.6 = (bf16[2,768,256]{2,1,0:T(8,128)(2,1)}, bf16[2,768,256]{2,1,0:T(8,128)(2,1)}, u32[]{:S(2)}, u32[]{:S(2)}) collective-permute-start(bf16[2,768,256]{2,1,0:T(8,128)(2,1)} %collective-permute-done.5), channel_id=1, source_target_pairs={{4,0},{8,4},{12,8},{16,12},{20,16},{24,20},{28,24},{32,28},{36,32}... | collective-permute-start | bytes 2359304 | tf_op jit(solution)/shard_map/ppermute | solution.py:16
  62.9 23.9 %collective-permute-start.3 = (bf16[2,384,256]{2,1,0:T(8,128)(2,1)}, bf16[2,384,256]{2,1,0:T(8,128)(2,1)}, u32[]{:S(2)}, u32[]{:S(2)}) collective-permute-start(bf16[2,384,256]{2,1,0:T(8,128)(2,1)} %collective-permute-done.2), channel_id=1, source_target_pairs={{0,4},{4,8},{8,12},{12,16},{16,20},{20,24},{24,28},{28,32},{32,36}... | collective-permute-start | bytes 1179656 | tf_op jit(solution)/shard_map/ppermute | solution.py:16
  94.2 25.2 %copy-start = (bf16[1,2,2,384,2,128]{5,4,3,2,1,0:T(2,128)(2,1)S(1)}, bf16[1,2,2,384,2,128]{5,4,3,2,1,0:T(2,128)(2,1)}, u32[]{:S(2)}) copy-start(bf16[1,2,2,384,2,128]{5,4,3,2,1,0:T(2,128)(2,1)} %stack.78) | copy-start | bytes 2359300
  99.5 24.9 %collective-permute-start.7 = (bf16[2,768,256]{2,1,0:T(8,128)(2,1)}, bf16[2,768,256]{2,1,0:T(8,128)(2,1)}, u32[]{:S(2)}, u32[]{:S(2)}) collective-permute-start(bf16[2,768,256]{2,1,0:T(8,128)(2,1)} %collective-permute-done.6), channel_id=1, source_target_pairs={{4,0},{8,4},{12,8},{16,12},{20,16},{24,20},{28,24},{32,28},{36,32}... | collective-permute-start | bytes 2359304 | tf_op jit(solution)/shard_map/ppermute | solution.py:16
where the time goes:
time: 308 us; the launch traced here: 307 us
  local copies, waits for them, and re-layouts  79.3 us (26%)
  starting transfers between devices  48 us (16%)
  matrix products  44 us (14%)
  loops' own time  42.1 us (14%)
  blocking collectives  37.7 us (12%)
  other arithmetic  30.1 us (10%)
  waiting for transfers between devices  25.4 us (8%)
    ppermute x8, starting transfers between devices, from_behind(): return lax.ppermute(block, axis, route)  48 us
    another operation x5, loops' own time, one_tile(): lax.cond(jnp.any(allowed), update, lambda state_old: state_old, state_now)  38.7 us
    all_to_all x1, blocking collectives, on_device(): lax.all_to_all(attended, 'tp', split_axis=0, concat_axis=1, tiled=True)  37.7 us
    dot_general x5, matrix products, update(): jnp.einsum('cqhjk,ckhd->cqhjd', weights.astype(jnp.bfloat16), pieces[:, 1...  33.8 us
    ppermute x8, waiting for transfers between devices, from_behind(): return lax.ppermute(block, axis, route)  25.4 us
    unnamed x15, local copies, waits for them, and re-layouts  24.7 us
    another operation x9, local copies, waits for them, and re-layouts, on_device(): kv_bank = jnp.stack(below_list[::-1] + [paired] + above_list)  16.8 us
    reduce_sum x5, other arithmetic, update(): new_sum = rescale * running_sum + jnp.sum(weights, axis=-1)  14.4 us
  transfers between devices with their start and end apart: 8, of which 3 were waited for; matrix products, arithmetic and copies ran while one was open for 16% of the time, Pallas kernels for 0%

commit v1 on v0

v1 whole, which is shorter than its diff:
```python
import functools
import math

import jax
import jax.numpy as jnp
from jax import lax
from jax.experimental import pallas as pl
from jax.experimental.pallas import tpu as pltpu
from jax.sharding import PartitionSpec as P

HEAD = 128
MESH = pl.DeviceIdType.MESH
MASKED = -1e30
KEY_TILE = 256


def other(bit):
    return 1 - bit


def kernel(sizes, lens_ref, q_hbm, k_hbm, v_hbm, out_hbm, kv, qbuf, bias, scores, outs,
           load_sem, q_sem, kv_send, kv_recv, out_send, out_recv, own_sem):
    cp_size, tp_size, half, groups, kv_local = sizes
    heads = groups * kv_local
    chunk = 2 * half // tp_size
    slots = 5
    window = bias.shape[-1]
    key_tiles = window // KEY_TILE
    cp = lax.axis_index("cp")
    tp = lax.axis_index("tp")
    core = cp % 2
    partner = cp + 1 - 2 * core

    def slot(direction, g, which):
        return kv.at[direction, g, :, pl.ds(which * half, half), :]

    at_end = [(cp >= cp_size - 2).astype(jnp.int32), (cp < 2).astype(jnp.int32)]
    beyond = [
        (1 - at_end[0]) * (cp + 2) + at_end[0] * partner,
        (1 - at_end[1]) * (cp - 2) + at_end[1] * partner,
    ]
    landing = [at_end[0], 1 - at_end[1]]
    is_lead = [core == 0, core == 1]
    lead_of = [1 - core, core]

    def load(direction, g, part):
        src = (k_hbm, v_hbm)[part]
        return pltpu.make_async_copy(
            src.at[pl.ds(direction * half, half), pl.ds(g * HEAD, HEAD)],
            kv.at[direction, g, part, pl.ds(4 * half, half), :],
            load_sem.at[direction, g, part],
        )

    def load_q(h):
        return pltpu.make_async_copy(
            q_hbm.at[:, pl.ds(h * HEAD, HEAD)], qbuf.at[h], q_sem.at[h]
        )

    def hop(direction, g, far):
        return pltpu.make_async_remote_copy(
            src_ref=slot(direction, g, 4 - 2 * far),
            dst_ref=slot(landing[direction], g, 2 - 2 * far),
            send_sem=kv_send.at[direction, g, far],
            recv_sem=kv_recv.at[landing[direction], g, 2 - 2 * far],
            device_id=(beyond[direction], tp),
            device_id_type=MESH,
        )

    def across(direction, g, far):
        lead = lead_of[direction]
        return pltpu.make_async_remote_copy(
            src_ref=slot(direction, g, 2 * lead + 2 - 2 * far),
            dst_ref=slot(direction, g, 3 - 2 * far),
            send_sem=kv_send.at[direction, g, 2 + far],
            recv_sem=kv_recv.at[direction, g, 3 - 2 * far],
            device_id=(partner, tp),
            device_id_type=MESH,
        )

    def arrived(direction, g, which):
        pltpu.make_async_remote_copy(
            src_ref=slot(direction, g, which),
            dst_ref=slot(direction, g, which),
            send_sem=kv_send.at[direction, g, 0],
            recv_sem=kv_recv.at[direction, g, which],
            device_id=(partner, tp),
            device_id_type=MESH,
        ).wait_recv()

    def peer_of(turn):
        n = 3 - turn
        high = (tp // 2 + n // 2) % 2
        low = (tp % 2 + n % 2 + n // 2) % 2
        return high, low

    def send(turn, h):
        high, low = peer_of(turn)
        return pltpu.make_async_remote_copy(
            src_ref=outs.at[turn, h],
            dst_ref=out_hbm.at[:, pl.ds((tp * heads + h) * HEAD, HEAD)],
            send_sem=out_send.at[turn, h],
            recv_sem=out_recv.at[turn, h],
            device_id=(cp, 2 * high + low),
            device_id_type=MESH,
        )

    def received(turn, h):
        high, low = peer_of(turn)
        return pltpu.make_async_remote_copy(
            src_ref=outs.at[turn, h],
            dst_ref=out_hbm.at[:, pl.ds(((2 * high + low) * heads + h) * HEAD, HEAD)],
            send_sem=out_send.at[turn, h],
            recv_sem=out_recv.at[turn, h],
            device_id=(cp, 2 * high + low),
            device_id_type=MESH,
        )

    def keep(h):
        return pltpu.make_async_copy(
            outs.at[3, h], out_hbm.at[:, pl.ds((tp * heads + h) * HEAD, HEAD)], own_sem.at[h]
        )

    for g in range(kv_local):
        for direction in range(2):
            for part in range(2):
                load(direction, g, part).start()
    for h in range(heads):
        load_q(h).start()

    barrier = pltpu.get_barrier_semaphore()
    for device in (beyond[0], beyond[1], partner):
        pl.semaphore_signal(barrier, inc=1, device_id=(device, tp), device_id_type=MESH)
    for turn in range(3):
        high, low = peer_of(turn)
        pl.semaphore_signal(barrier, inc=1, device_id=(cp, 2 * high + low), device_id_type=MESH)
    pl.semaphore_wait(barrier, 6)

    for g in range(kv_local):
        for direction in range(2):
            load(direction, g, 0).wait()
            load(direction, g, 1).wait()
            hop(direction, g, 0).start()

            @pl.when(is_lead[direction])
            def _():
                across(direction, g, 0).start()

    row = lax.broadcasted_iota(jnp.int32, (HEAD, HEAD), 0)
    col = lax.broadcasted_iota(jnp.int32, (HEAD, HEAD), 1)
    upper = (row <= col).astype(jnp.float32)
    lens = jnp.broadcast_to(lens_ref[...], (8, HEAD))
    ends = jnp.dot(lens, upper, precision=lax.Precision.HIGHEST, preferred_element_type=jnp.float32)[:1]
    lens = lens[:1]
    for turn in range(4):
        high, low = peer_of(turn)
        block = high * (2 * cp_size - 1 - 2 * cp) + cp
        q_pos = (
            lax.broadcasted_iota(jnp.int32, (chunk, 1), 0) + (block * half + low * chunk)
        ).astype(jnp.float32)
        start = jnp.sum(jnp.where(ends <= q_pos, lens, 0.0), axis=1, keepdims=True)
        for n in range(key_tiles):
            k_pos = (
                lax.broadcasted_iota(jnp.int32, (1, KEY_TILE), 1)
                + ((block - 4) * half + low * HEAD + n * KEY_TILE)
            ).astype(jnp.float32)
            allowed = (k_pos >= start) & (k_pos <= q_pos)
            bias[turn, :, n * KEY_TILE : (n + 1) * KEY_TILE] = jnp.where(allowed, 0.0, MASKED)

    for h in range(heads):
        load_q(h).wait()

    for g in range(kv_local):
        for direction in range(2):
            arrived(direction, g, 2)
            hop(direction, g, 1).start()

            @pl.when(is_lead[direction])
            def _():
                across(direction, g, 1).start()

            @pl.when(is_lead[1 - direction])
            def _():
                across(direction, g, 0).start()

    def complete(g):
        for direction in range(2):
            arrived(direction, g, 0)

            @pl.when(is_lead[1 - direction])
            def _():
                across(direction, g, 1).start()

        for direction in range(2):
            arrived(direction, g, 3)
            arrived(direction, g, 1)

    complete(0)

    factor = math.log2(math.e) / math.sqrt(HEAD)

    def unit(u, carry):
        later = u // 4
        turn = (1 - later) * (u % 2) + later * (2 + (u % 4) // 2)
        g = (1 - later) * (u // 2) + later * (u % 2)
        direction, low = peer_of(turn)
        q_start = pl.multiple_of(direction * half + low * chunk, 64)
        k_start = pl.multiple_of(low * HEAD, HEAD)

        @pl.when(u == 2)
        def _():
            for later_g in range(1, kv_local):
                complete(later_g)

        def scores_tile(h, n):
            q = qbuf[g * groups + h, pl.ds(q_start, chunk), :]
            k = kv[direction, g, 0, pl.ds(k_start + n * KEY_TILE, KEY_TILE), :]
            s = lax.dot_general(q, k, (((1,), (1,)), ((), ())), preferred_element_type=jnp.float32)
            s = s * factor + bias[turn, :, n * KEY_TILE : (n + 1) * KEY_TILE]
            scores[h % 2, :, n * KEY_TILE : (n + 1) * KEY_TILE] = s
            return jnp.maximum(s[:, :HEAD], s[:, HEAD:])

        def value_tile(h, n, top):
            p = jnp.exp2(scores[h % 2, :, n * KEY_TILE : (n + 1) * KEY_TILE] - top)
            v = kv[direction, g, 1, pl.ds(k_start + n * KEY_TILE, KEY_TILE), :]
            product = jnp.dot(p.astype(jnp.bfloat16), v, preferred_element_type=jnp.float32)
            return product, p[:, :HEAD] + p[:, HEAD:]

        highest = scores_tile(0, 0)
        for n in range(1, key_tiles):
            highest = jnp.maximum(highest, scores_tile(0, n))
        for h in range(groups):
            top = jnp.max(highest, axis=1, keepdims=True)
            total = weight = highest = None
            for n in range(key_tiles):
                if h + 1 < groups:
                    tile = scores_tile(h + 1, n)
                    highest = tile if highest is None else jnp.maximum(highest, tile)
                product, part = value_tile(h, n, top)
                total = product if total is None else total + product
                weight = part if weight is None else weight + part
            weight = jnp.sum(weight, axis=1, keepdims=True)
            outs[turn, g * groups + h] = (total / weight).astype(outs.dtype)
            if h > 0:
                ship(turn, g * groups + h - 1)
        ship(turn, g * groups + groups - 1)
        return carry

    def ship(turn, h):
        @pl.when(turn < 3)
        def _():
            send(turn, h).start()

        @pl.when(turn == 3)
        def _():
            keep(h).start()

    lax.fori_loop(0, 4 * kv_local, unit, 0)

    for g in range(kv_local):
        for direction in range(2):
            for far in range(2):
                hop(direction, g, far).wait_send()
                across(direction, g, far).wait_send()

    def drain(i, carry):
        turn, h = i // heads, i % heads
        send(turn, h).wait_send()
        received(turn, h).wait_recv()
        return carry

    lax.fori_loop(0, 3 * heads, drain, 0)
    for h in range(heads):
        keep(h).wait()


def on_device(cp_size, tp_size, queries, keys, values, doc_lengths):
    tok_rows, q_cols = queries.shape
    half = tok_rows // 2
    kv_local = keys.shape[1] // HEAD
    heads = q_cols // HEAD
    groups = heads // kv_local
    chunk = tok_rows // tp_size
    window = 7 * KEY_TILE
    lens = jnp.pad(doc_lengths.astype(jnp.float32), (0, HEAD - doc_lengths.shape[0]))[None]
    hbm = pl.BlockSpec(memory_space=pl.ANY)
    return pl.pallas_call(
        functools.partial(kernel, (cp_size, tp_size, half, groups, kv_local)),
        out_shape=jax.ShapeDtypeStruct((chunk, q_cols * tp_size), jnp.bfloat16),
        in_specs=[pl.BlockSpec(memory_space=pltpu.VMEM), hbm, hbm, hbm],
        out_specs=hbm,
        scratch_shapes=[
            pltpu.VMEM((2, kv_local, 2, 5 * half, HEAD), jnp.bfloat16),
            pltpu.VMEM((heads, tok_rows, HEAD), jnp.bfloat16),
            pltpu.VMEM((4, chunk, window), jnp.float32),
            pltpu.VMEM((2, chunk, window), jnp.float32),
            pltpu.VMEM((4, heads, chunk, HEAD), jnp.bfloat16),
            pltpu.SemaphoreType.DMA((2, kv_local, 2)),
            pltpu.SemaphoreType.DMA((heads,)),
            pltpu.SemaphoreType.DMA((2, kv_local, 4)),
            pltpu.SemaphoreType.DMA((2, kv_local, 4)),
            pltpu.SemaphoreType.DMA((3, heads)),
            pltpu.SemaphoreType.DMA((3, heads)),
            pltpu.SemaphoreType.DMA((heads,)),
        ],
        compiler_params=pltpu.CompilerParams(
            collective_id=0, has_side_effects=True, vmem_limit_bytes=60 * 1024 * 1024
        ),
    )(lens, queries, keys, values)


def solution(mesh):
    in_specs = (P("cp", "tp"), P("cp", "tp"), P("cp", "tp"), P())
    out_specs = P(("cp", "tp"), None)
    return jax.shard_map(
        functools.partial(on_device, mesh.shape["cp"], mesh.shape["tp"]),
        mesh=mesh, in_specs=in_specs, out_specs=out_specs, check_vma=False,
    )
```

time: 308 us -> 91.3 us (0.30)
  the two profiles are of different devices: /device:TPU:128 before, /device:TPU:63 now
where the time goes in v1:
time: 91.3 us; the launch traced here: 91.1 us
  Pallas kernels  87 us (95%)
  local copies, waits for them, and re-layouts  3.46 us (4%)
    pallas_call x1, Pallas kernels, on_device(): pl.pallas_call(functools.partial(kernel, (cp_size, tp_size, half, groups,...  87 us
    unnamed x1, local copies, waits for them, and re-layouts  2.94 us

profile of v1, /device:TPU:63, one launch (start us, length us, event | category | flops | bytes accessed | tf_op | source)
XLA Modules:
  0.0 91.1 jit_solution(6941912511230147219)
XLA Ops:
  0.0 0.7 convert_element_type.5
  0.7 0.5 pad_bitcast_fusion.lens_ref
  1.2 87.0 %shard_map.46 = bf16[192,5120]{1,0:T(8,128)(2,1)} custom-call(f32[1,128]{1,0:T(1,128)} %pad_bitcast_fusion.lens_ref, bf16[768,1280]{1,0:T(8,128)(2,1)} %q_hbm.1, bf16[768,256]{1,0:T(8,128)(2,1)} %k_hbm.1, bf16[768,256]{1,0:T(8,128)(2,1)} %v_hbm.1), custom_call_target="tpu_custom_call" | custom-call | tf_op jit(solution)/shard_map/pallas_call | solution.py:286
  88.2 2.9 %copy.6 = bf16[192,5120]{1,0:T(8,128)(2,1)} copy(bf16[192,5120]{1,0:T(8,128)(2,1)} %shard_map.46) | data formatting | bytes 3932160

commit v2 on v1

--- a/solution.py
+++ b/solution.py
@@ -14,16 +14,11 @@
 KEY_TILE = 256
 
 
-def other(bit):
-    return 1 - bit
-
-
 def kernel(sizes, lens_ref, q_hbm, k_hbm, v_hbm, out_hbm, kv, qbuf, bias, scores, outs,
-           load_sem, q_sem, kv_send, kv_recv, out_send, out_recv, own_sem):
+           load_sem, q_sem, kv_send, leap_send, kv_recv, out_send, out_recv, own_sem):
     cp_size, tp_size, half, groups, kv_local = sizes
     heads = groups * kv_local
     chunk = 2 * half // tp_size
-    slots = 5
     window = bias.shape[-1]
     key_tiles = window // KEY_TILE
     cp = lax.axis_index("cp")
@@ -31,8 +26,8 @@
     core = cp % 2
     partner = cp + 1 - 2 * core
 
-    def slot(direction, g, which):
-        return kv.at[direction, g, :, pl.ds(which * half, half), :]
+    def slot(direction, g, part, which):
+        return kv.at[direction, g, part, pl.ds(which * half, half), :]
 
     at_end = [(cp >= cp_size - 2).astype(jnp.int32), (cp < 2).astype(jnp.int32)]
     beyond = [
@@ -43,11 +38,21 @@
     is_lead = [core == 0, core == 1]
     lead_of = [1 - core, core]
 
+    chips = cp_size // 2
+    chip = cp // 2
+    middle = chips // 2
+    stops = [chip == middle - 1, chip == middle]
+    leaps = [chip == middle - 2, chip == middle + 1]
+    leap_to = [cp + 4, cp - 4]
+    near_gap = (chip >= middle - 2) & (chip <= middle + 1)
+    below_gap = (chip < middle).astype(jnp.int32)
+    mate = cp - 4 + 8 * below_gap
+
     def load(direction, g, part):
         src = (k_hbm, v_hbm)[part]
         return pltpu.make_async_copy(
             src.at[pl.ds(direction * half, half), pl.ds(g * HEAD, HEAD)],
-            kv.at[direction, g, part, pl.ds(4 * half, half), :],
+            slot(direction, g, part, 4),
             load_sem.at[direction, g, part],
         )
 
@@ -56,36 +61,87 @@
             q_hbm.at[:, pl.ds(h * HEAD, HEAD)], qbuf.at[h], q_sem.at[h]
         )
 
-    def hop(direction, g, far):
-        return pltpu.make_async_remote_copy(
-            src_ref=slot(direction, g, 4 - 2 * far),
-            dst_ref=slot(landing[direction], g, 2 - 2 * far),
-            send_sem=kv_send.at[direction, g, far],
-            recv_sem=kv_recv.at[landing[direction], g, 2 - 2 * far],
+    def hop(direction, g, part, far):
+        return pltpu.make_async_remote_copy(
+            src_ref=slot(direction, g, part, 4 - 2 * far),
+            dst_ref=slot(landing[direction], g, part, 2 - 2 * far),
+            send_sem=kv_send.at[direction, g, part, far],
+            recv_sem=kv_recv.at[landing[direction], g, part, 2 - 2 * far],
             device_id=(beyond[direction], tp),
             device_id_type=MESH,
         )
 
-    def across(direction, g, far):
+    def leap(direction, g, part):
+        return pltpu.make_async_remote_copy(
+            src_ref=slot(direction, g, part, 4),
+            dst_ref=slot(direction, g, part, 0),
+            send_sem=leap_send.at[direction, g, part],
+            recv_sem=kv_recv.at[direction, g, part, 0],
+            device_id=(leap_to[direction], tp),
+            device_id_type=MESH,
+        )
+
+    def across(direction, g, part, far):
         lead = lead_of[direction]
         return pltpu.make_async_remote_copy(
-            src_ref=slot(direction, g, 2 * lead + 2 - 2 * far),
-            dst_ref=slot(direction, g, 3 - 2 * far),
-            send_sem=kv_send.at[direction, g, 2 + far],
-            recv_sem=kv_recv.at[direction, g, 3 - 2 * far],
+            src_ref=slot(direction, g, part, 2 * lead + 2 - 2 * far),
+            dst_ref=slot(direction, g, part, 3 - 2 * far),
+            send_sem=kv_send.at[direction, g, part, 2 + far],
+            recv_sem=kv_recv.at[direction, g, part, 3 - 2 * far],
             device_id=(partner, tp),
             device_id_type=MESH,
         )
 
-    def arrived(direction, g, which):
+    def arrived(direction, g, part, which):
         pltpu.make_async_remote_copy(
-            src_ref=slot(direction, g, which),
-            dst_ref=slot(direction, g, which),
-            send_sem=kv_send.at[direction, g, 0],
-            recv_sem=kv_recv.at[direction, g, which],
+            src_ref=slot(direction, g, part, which),
+            dst_ref=slot(direction, g, part, which),
+            send_sem=kv_send.at[direction, g, part, 0],
+            recv_sem=kv_recv.at[direction, g, part, which],
             device_id=(partner, tp),
             device_id_type=MESH,
         ).wait_recv()
+
+    def offer(g, part):
+        for direction in range(2):
+            load(direction, g, part).wait()
+            hop(direction, g, part, 0).start()
+
+            @pl.when(leaps[direction])
+            def _():
+                leap(direction, g, part).start()
+
+            @pl.when(is_lead[direction])
+            def _():
+                across(direction, g, part, 0).start()
+
+    def relay(g, part):
+        for direction in range(2):
+            arrived(direction, g, part, 2)
+
+            @pl.when(jnp.logical_not(stops[direction]))
+            def _():
+                hop(direction, g, part, 1).start()
+
+            @pl.when(is_lead[direction])
+            def _():
+                across(direction, g, part, 1).start()
+
+            @pl.when(is_lead[1 - direction])
+            def _():
+                across(direction, g, part, 0).start()
+
+    def complete(g, part):
+        for direction in range(2):
+            arrived(direction, g, part, 0)
+
+            @pl.when(is_lead[1 - direction])
+            def _():
+                across(direction, g, part, 1).start()
+
+        for direction in range(2):
+            arrived(direction, g, part, 3)
+            arrived(direction, g, part, 1)
 
     def peer_of(turn):
         n = 3 - turn
@@ -120,30 +176,28 @@
             outs.at[3, h], out_hbm.at[:, pl.ds((tp * heads + h) * HEAD, HEAD)], own_sem.at[h]
         )
 
+    barrier = pltpu.get_barrier_semaphore()
+    for turn in range(3):
+        high, low = peer_of(turn)
+        pl.semaphore_signal(barrier, inc=1, device_id=(cp, 2 * high + low), device_id_type=MESH)
+    for device in (beyond[0], beyond[1], partner):
+        pl.semaphore_signal(barrier, inc=1, device_id=(device, tp), device_id_type=MESH)
+
+    @pl.when(near_gap)
+    def _():
+        pl.semaphore_signal(barrier, inc=1, device_id=(mate, tp), device_id_type=MESH)
+
     for g in range(kv_local):
-        for direction in range(2):
-            for part in range(2):
+        for part in range(2):
+            for direction in range(2):
                 load(direction, g, part).start()
     for h in range(heads):
         load_q(h).start()
 
-    barrier = pltpu.get_barrier_semaphore()
-    for device in (beyond[0], beyond[1], partner):
-        pl.semaphore_signal(barrier, inc=1, device_id=(device, tp), device_id_type=MESH)
-    for turn in range(3):
-        high, low = peer_of(turn)
-        pl.semaphore_signal(barrier, inc=1, device_id=(cp, 2 * high + low), device_id_type=MESH)
-    pl.semaphore_wait(barrier, 6)
-
-    for g in range(kv_local):
-        for direction in range(2):
-            load(direction, g, 0).wait()
-            load(direction, g, 1).wait()
-            hop(direction, g, 0).start()
-
-            @pl.when(is_lead[direction])
-            def _():
-                across(direction, g, 0).start()
+    pl.semaphore_wait(barrier, 6 + near_gap.astype(jnp.int32))
+
+    offer(0, 0)
+    offer(0, 1)
 
     row = lax.broadcasted_iota(jnp.int32, (HEAD, HEAD), 0)
     col = lax.broadcasted_iota(jnp.int32, (HEAD, HEAD), 1)
@@ -169,47 +223,46 @@
     for h in range(heads):
         load_q(h).wait()
 
-    for g in range(kv_local):
-        for direction in range(2):
-            arrived(direction, g, 2)
-            hop(direction, g, 1).start()
-
-            @pl.when(is_lead[direction])
-            def _():
-                across(direction, g, 1).start()
-
-            @pl.when(is_lead[1 - direction])
-            def _():
-                across(direction, g, 0).start()
-
-    def complete(g):
-        for direction in range(2):
-            arrived(direction, g, 0)
-
-            @pl.when(is_lead[1 - direction])
-            def _():
-                across(direction, g, 1).start()
-
-        for direction in range(2):
-            arrived(direction, g, 3)
-            arrived(direction, g, 1)
-
-    complete(0)
+    relay(0, 0)
+    relay(0, 1)
+    for g in range(1, kv_local):
+        offer(g, 0)
+        offer(g, 1)
+    complete(0, 0)
+    complete(0, 1)
 
     factor = math.log2(math.e) / math.sqrt(HEAD)
 
-    def unit(u, carry):
+    def ship(turn, h):
+        @pl.when(turn < 3)
+        def _():
+            send(turn, h).start()
+
+        @pl.when(turn == 3)
+        def _():
+            keep(h).start()
+
+    def place(u):
         later = u // 4
         turn = (1 - later) * (u % 2) + later * (2 + (u % 4) // 2)
         g = (1 - later) * (u // 2) + later * (u % 2)
+        return turn, g
+
+    def unit(u, carry):
+        turn, g = place(u)
         direction, low = peer_of(turn)
         q_start = pl.multiple_of(direction * half + low * chunk, 64)
         k_start = pl.multiple_of(low * HEAD, HEAD)
 
+        @pl.when(u == 1)
+        def _():
+            relay(1, 0)
+
         @pl.when(u == 2)
         def _():
-            for later_g in range(1, kv_local):
-                complete(later_g)
+            relay(1, 1)
+            complete(1, 0)
+            complete(1, 1)
 
         def scores_tile(h, n):
             q = qbuf[g * groups + h, pl.ds(q_start, chunk), :]
@@ -228,6 +281,12 @@
         highest = scores_tile(0, 0)
         for n in range(1, key_tiles):
             highest = jnp.maximum(highest, scores_tile(0, n))
+
+        @pl.when(u > 0)
+        def _():
+            last_turn, last_g = place(u - 1)
+            ship(last_turn, last_g * groups + groups - 1)
+
         for h in range(groups):
             top = jnp.max(highest, axis=1, keepdims=True)
             total = weight = highest = None
@@ -242,25 +301,26 @@
             outs[turn, g * groups + h] = (total / weight).astype(outs.dtype)
             if h > 0:
                 ship(turn, g * groups + h - 1)
-        ship(turn, g * groups + groups - 1)
         return carry
 
-    def ship(turn, h):
-        @pl.when(turn < 3)
-        def _():
-            send(turn, h).start()
-
-        @pl.when(turn == 3)
-        def _():
-            keep(h).start()
-
     lax.fori_loop(0, 4 * kv_local, unit, 0)
 
+    keep(heads - 1).start()
+
     for g in range(kv_local):
-        for direction in range(2):
-            for far in range(2):
-                hop(direction, g, far).wait_send()
-                across(direction, g, far).wait_send()
+        for part in range(2):
+            for direction in range(2):
+                hop(direction, g, part, 0).wait_send()
+                across(direction, g, part, 0).wait_send()
+                across(direction, g, part, 1).wait_send()
+
+                @pl.when(jnp.logical_not(stops[direction]))
+                def _():
+                    hop(direction, g, part, 1).wait_send()
+
+                @pl.when(leaps[direction])
+                def _():
+                    leap(direction, g, part).wait_send()
 
     def drain(i, carry):
         turn, h = i // heads, i % heads
@@ -296,8 +356,9 @@
             pltpu.VMEM((4, heads, chunk, HEAD), jnp.bfloat16),
             pltpu.SemaphoreType.DMA((2, kv_local, 2)),
             pltpu.SemaphoreType.DMA((heads,)),
-            pltpu.SemaphoreType.DMA((2, kv_local, 4)),
-            pltpu.SemaphoreType.DMA((2, kv_local, 4)),
+            pltpu.SemaphoreType.DMA((2, kv_local, 2, 4)),
+            pltpu.SemaphoreType.DMA((2, kv_local, 2)),
+            pltpu.SemaphoreType.DMA((2, kv_local, 2, 4)),
             pltpu.SemaphoreType.DMA((3, heads)),
             pltpu.SemaphoreType.DMA((3, heads)),
             pltpu.SemaphoreType.DMA((heads,)),

time: 91.3 us -> 80.2 us (0.88)
  the two profiles are of different devices: /device:TPU:63 before, /device:TPU:29 now
where the time goes in v2:
time: 80.2 us; the launch traced here: 80 us
  Pallas kernels  75.9 us (95%)
  local copies, waits for them, and re-layouts  3.46 us (4%)
    pallas_call x1, Pallas kernels, on_device(): pl.pallas_call(functools.partial(kernel, (cp_size, tp_size, half, groups,...  75.9 us
    unnamed x1, local copies, waits for them, and re-layouts  2.94 us

profile of v2, /device:TPU:29, one launch (start us, length us, event | category | flops | bytes accessed | tf_op | source)
XLA Modules:
  0.0 80.0 jit_solution(9185115900170061695)
XLA Ops:
  0.0 0.7 convert_element_type.5
  0.7 0.5 pad_bitcast_fusion.lens_ref
  1.2 75.9 %shard_map.46 = bf16[192,5120]{1,0:T(8,128)(2,1)} custom-call(f32[1,128]{1,0:T(1,128)} %pad_bitcast_fusion.lens_ref, bf16[768,1280]{1,0:T(8,128)(2,1)} %q_hbm.1, bf16[768,256]{1,0:T(8,128)(2,1)} %k_hbm.1, bf16[768,256]{1,0:T(8,128)(2,1)} %v_hbm.1), custom_call_target="tpu_custom_call" | custom-call | tf_op jit(solution)/shard_map/pallas_call | solution.py:346
  77.1 2.9 %copy.6 = bf16[192,5120]{1,0:T(8,128)(2,1)} copy(bf16[192,5120]{1,0:T(8,128)(2,1)} %shard_map.46) | data formatting | bytes 3932160

commit v3 on v2

--- a/solution.py
+++ b/solution.py
@@ -25,33 +25,45 @@
     tp = lax.axis_index("tp")
     core = cp % 2
     partner = cp + 1 - 2 * core
+    far_way = 1 - tp // 2
+    near_way = tp // 2
 
     def slot(direction, g, part, which):
         return kv.at[direction, g, part, pl.ds(which * half, half), :]
 
-    at_end = [(cp >= cp_size - 2).astype(jnp.int32), (cp < 2).astype(jnp.int32)]
-    beyond = [
-        (1 - at_end[0]) * (cp + 2) + at_end[0] * partner,
-        (1 - at_end[1]) * (cp - 2) + at_end[1] * partner,
-    ]
-    landing = [at_end[0], 1 - at_end[1]]
-    is_lead = [core == 0, core == 1]
-    lead_of = [1 - core, core]
+    at_top = (cp >= cp_size - 2).astype(jnp.int32)
+    at_bottom = (cp < 2).astype(jnp.int32)
+    is_end = ((cp < 2) & (far_way == 0)) | ((cp >= cp_size - 2) & (far_way == 1))
+    above = (1 - at_top) * (cp + 2) + at_top * partner
+    below = (1 - at_bottom) * (cp - 2) + at_bottom * partner
 
     chips = cp_size // 2
     chip = cp // 2
     middle = chips // 2
-    stops = [chip == middle - 1, chip == middle]
-    leaps = [chip == middle - 2, chip == middle + 1]
-    leap_to = [cp + 4, cp - 4]
     near_gap = (chip >= middle - 2) & (chip <= middle + 1)
     below_gap = (chip < middle).astype(jnp.int32)
     mate = cp - 4 + 8 * below_gap
+    near_first = near_gap & (near_way == 1 - below_gap)
+
+    def beyond(direction):
+        return (1 - direction) * above + direction * below
+
+    def landing(direction):
+        return (1 - direction) * at_top + direction * (1 - at_bottom)
+
+    def lead(direction):
+        return (1 - core) * (1 - direction) + core * direction
+
+    def stops(direction):
+        return chip == middle - 1 + direction
+
+    def leaps(direction):
+        return chip == middle - 2 + 3 * direction
 
     def load(direction, g, part):
         src = (k_hbm, v_hbm)[part]
         return pltpu.make_async_copy(
-            src.at[pl.ds(direction * half, half), pl.ds(g * HEAD, HEAD)],
+            src.at[pl.ds(pl.multiple_of(direction * half, half), half), pl.ds(g * HEAD, HEAD)],
             slot(direction, g, part, 4),
             load_sem.at[direction, g, part],
         )
@@ -64,10 +76,10 @@
     def hop(direction, g, part, far):
         return pltpu.make_async_remote_copy(
             src_ref=slot(direction, g, part, 4 - 2 * far),
-            dst_ref=slot(landing[direction], g, part, 2 - 2 * far),
+            dst_ref=slot(landing(direction), g, part, 2 - 2 * far),
             send_sem=kv_send.at[direction, g, part, far],
-            recv_sem=kv_recv.at[landing[direction], g, part, 2 - 2 * far],
-            device_id=(beyond[direction], tp),
+            recv_sem=kv_recv.at[landing(direction), g, part, 2 - 2 * far],
+            device_id=(beyond(direction), tp),
             device_id_type=MESH,
         )
 
@@ -77,14 +89,13 @@
             dst_ref=slot(direction, g, part, 0),
             send_sem=leap_send.at[direction, g, part],
             recv_sem=kv_recv.at[direction, g, part, 0],
-            device_id=(leap_to[direction], tp),
+            device_id=(cp + 4 - 8 * direction, tp),
             device_id_type=MESH,
         )
 
     def across(direction, g, part, far):
-        lead = lead_of[direction]
         return pltpu.make_async_remote_copy(
-            src_ref=slot(direction, g, part, 2 * lead + 2 - 2 * far),
+            src_ref=slot(direction, g, part, 2 * lead(direction) + 2 - 2 * far),
             dst_ref=slot(direction, g, part, 3 - 2 * far),
             send_sem=kv_send.at[direction, g, part, 2 + far],
             recv_sem=kv_recv.at[direction, g, part, 3 - 2 * far],
@@ -102,46 +113,42 @@
             device_id_type=MESH,
         ).wait_recv()
 
-    def offer(g, part):
-        for direction in range(2):
-            load(direction, g, part).wait()
-            hop(direction, g, part, 0).start()
-
-            @pl.when(leaps[direction])
-            def _():
-                leap(direction, g, part).start()
-
-            @pl.when(is_lead[direction])
-            def _():
-                across(direction, g, part, 0).start()
-
-    def relay(g, part):
-        for direction in range(2):
-            arrived(direction, g, part, 2)
-
-            @pl.when(jnp.logical_not(stops[direction]))
-            def _():
-                hop(direction, g, part, 1).start()
-
-            @pl.when(is_lead[direction])
-            def _():
-                across(direction, g, part, 1).start()
-
-            @pl.when(is_lead[1 - direction])
-            def _():
-                across(direction, g, part, 0).start()
-
-    def complete(g, part):
-        for direction in range(2):
-            arrived(direction, g, part, 0)
-
-            @pl.when(is_lead[1 - direction])
-            def _():
-                across(direction, g, part, 1).start()
-
-        for direction in range(2):
-            arrived(direction, g, part, 3)
-            arrived(direction, g, part, 1)
+    def offer(direction, g, part):
+        load(direction, g, part).wait()
+        hop(direction, g, part, 0).start()
+
+        @pl.when(leaps(direction))
+        def _():
+            leap(direction, g, part).start()
+
+        @pl.when(lead(direction) == 1)
+        def _():
+            across(direction, g, part, 0).start()
+
+    def relay(direction, g, part):
+        arrived(direction, g, part, 2)
+
+        @pl.when(jnp.logical_not(stops(direction)))
+        def _():
+            hop(direction, g, part, 1).start()
+
+        @pl.when(lead(direction) == 1)
+        def _():
+            across(direction, g, part, 1).start()
+
+        @pl.when(lead(direction) == 0)
+        def _():
+            across(direction, g, part, 0).start()
+
+    def complete(direction, g, part):
+        arrived(direction, g, part, 0)
+
+        @pl.when(lead(direction) == 0)
+        def _():
+            across(direction, g, part, 1).start()
+
+        arrived(direction, g, part, 3)
+        arrived(direction, g, part, 1)
 
     def peer_of(turn):
         n = 3 - turn
@@ -180,29 +187,39 @@
     for turn in range(3):
         high, low = peer_of(turn)
         pl.semaphore_signal(barrier, inc=1, device_id=(cp, 2 * high + low), device_id_type=MESH)
-    for device in (beyond[0], beyond[1], partner):
+    for device in (above, below, partner):
         pl.semaphore_signal(barrier, inc=1, device_id=(device, tp), device_id_type=MESH)
 
     @pl.when(near_gap)
     def _():
         pl.semaphore_signal(barrier, inc=1, device_id=(mate, tp), device_id_type=MESH)
 
-    for g in range(kv_local):
-        for part in range(2):
-            for direction in range(2):
+    for direction in (far_way, near_way):
+        for g in range(kv_local):
+            for part in range(2):
                 load(direction, g, part).start()
     for h in range(heads):
         load_q(h).start()
 
     pl.semaphore_wait(barrier, 6 + near_gap.astype(jnp.int32))
 
-    offer(0, 0)
-    offer(0, 1)
+    offer(far_way, 0, 0)
+    offer(far_way, 0, 1)
+
+    @pl.when(jnp.logical_not(near_gap))
+    def _():
+        offer(near_way, 0, 0)
+        offer(near_way, 0, 1)
+
 
     row = lax.broadcasted_iota(jnp.int32, (HEAD, HEAD), 0)
     col = lax.broadcasted_iota(jnp.int32, (HEAD, HEAD), 1)
     upper = (row <= col).astype(jnp.float32)
-    lens = jnp.broadcast_to(lens_ref[...], (8, HEAD))
+    docs = lens_ref.shape[-1]
+    lens = jnp.concatenate(
+        [lens_ref[...].reshape(1, docs).astype(jnp.float32), jnp.zeros((1, HEAD - docs), jnp.float32)], axis=1
+    )
+    lens = jnp.broadcast_to(lens, (8, HEAD))
     ends = jnp.dot(lens, upper, precision=lax.Precision.HIGHEST, preferred_element_type=jnp.float32)[:1]
     lens = lens[:1]
     for turn in range(4):
@@ -223,13 +240,34 @@
     for h in range(heads):
         load_q(h).wait()
 
-    relay(0, 0)
-    relay(0, 1)
-    for g in range(1, kv_local):
-        offer(g, 0)
-        offer(g, 1)
-    complete(0, 0)
-    complete(0, 1)
+    @pl.when(near_gap)
+    def _():
+        hop(far_way, 0, 1, 0).wait_send()
+        for way, g in ((near_way, 0), (far_way, 1), (near_way, 1)):
+            offer(way, g, 0)
+            offer(way, g, 1)
+
+    @pl.when(near_first)
+    def _():
+        for g in range(kv_local):
+            relay(near_way, g, 0)
+            relay(near_way, g, 1)
+
+    relay(far_way, 0, 0)
+    relay(far_way, 0, 1)
+
+    @pl.when(jnp.logical_not(near_gap))
+    def _():
+        for way in (far_way, near_way):
+            offer(way, 1, 0)
+            offer(way, 1, 1)
+
+    @pl.when(is_end)
+    def _():
+        relay(near_way, 0, 0)
+        relay(near_way, 0, 1)
+
+    complete(far_way, 0, 0)
 
     factor = math.log2(math.e) / math.sqrt(HEAD)
 
@@ -243,10 +281,7 @@
             keep(h).start()
 
     def place(u):
-        later = u // 4
-        turn = (1 - later) * (u % 2) + later * (2 + (u % 4) // 2)
-        g = (1 - later) * (u // 2) + later * (u % 2)
-        return turn, g
+        return 2 * (u // 4) + u % 2, (u // 2) % 2
 
     def unit(u, carry):
         turn, g = place(u)
@@ -256,13 +291,38 @@
 
         @pl.when(u == 1)
         def _():
-            relay(1, 0)
+            relay(far_way, 1, 0)
+            relay(far_way, 1, 1)
 
         @pl.when(u == 2)
         def _():
-            relay(1, 1)
-            complete(1, 0)
-            complete(1, 1)
+            @pl.when(is_end)
+            def _():
+                relay(near_way, 1, 0)
+                relay(near_way, 1, 1)
+
+            complete(far_way, 1, 0)
+            complete(far_way, 1, 1)
+
+            @pl.when(jnp.logical_not(is_end | near_first))
+            def _():
+                relay(near_way, 0, 0)
+                relay(near_way, 0, 1)
+
+        @pl.when((u == 3) & jnp.logical_not(is_end | near_first))
+        def _():
+            relay(near_way, 1, 0)
+            relay(near_way, 1, 1)
+
+        @pl.when(u == 4)
+        def _():
+            complete(near_way, 0, 0)
+            complete(near_way, 0, 1)
+
+        @pl.when(u == 6)
+        def _():
+            complete(near_way, 1, 0)
+            complete(near_way, 1, 1)
 
         def scores_tile(h, n):
             q = qbuf[g * groups + h, pl.ds(q_start, chunk), :]
@@ -281,6 +341,10 @@
         highest = scores_tile(0, 0)
         for n in range(1, key_tiles):
             highest = jnp.maximum(highest, scores_tile(0, n))
+
+        @pl.when(u == 0)
+        def _():
+            complete(far_way, 0, 1)
 
         @pl.when(u > 0)
         def _():
@@ -309,18 +373,25 @@
 
     for g in range(kv_local):
         for part in range(2):
-            for direction in range(2):
-                hop(direction, g, part, 0).wait_send()
-                across(direction, g, part, 0).wait_send()
-                across(direction, g, part, 1).wait_send()
-
-                @pl.when(jnp.logical_not(stops[direction]))
+            for way in (far_way, near_way):
+                if g == 0 and part == 1 and way is far_way:
+
+                    @pl.when(jnp.logical_not(near_gap))
+                    def _():
+                        hop(way, g, part, 0).wait_send()
+
+                else:
+                    hop(way, g, part, 0).wait_send()
+                across(way, g, part, 0).wait_send()
+                across(way, g, part, 1).wait_send()
+
+                @pl.when(jnp.logical_not(stops(way)))
                 def _():
-                    hop(direction, g, part, 1).wait_send()
-
-                @pl.when(leaps[direction])
+                    hop(way, g, part, 1).wait_send()
+
+                @pl.when(leaps(way))
                 def _():
-                    leap(direction, g, part).wait_send()
+                    leap(way, g, part).wait_send()
 
     def drain(i, carry):
         turn, h = i // heads, i % heads
@@ -341,13 +412,12 @@
     groups = heads // kv_local
     chunk = tok_rows // tp_size
     window = 7 * KEY_TILE
-    lens = jnp.pad(doc_lengths.astype(jnp.float32), (0, HEAD - doc_lengths.shape[0]))[None]
     hbm = pl.BlockSpec(memory_space=pl.ANY)
     return pl.pallas_call(
         functools.partial(kernel, (cp_size, tp_size, half, groups, kv_local)),
-        out_shape=jax.ShapeDtypeStruct((chunk, q_cols * tp_size), jnp.bfloat16),
+        out_shape=pltpu.VMEM((chunk, q_cols * tp_size), jnp.bfloat16),
         in_specs=[pl.BlockSpec(memory_space=pltpu.VMEM), hbm, hbm, hbm],
-        out_specs=hbm,
+        out_specs=pl.BlockSpec(memory_space=pltpu.VMEM),
         scratch_shapes=[
             pltpu.VMEM((2, kv_local, 2, 5 * half, HEAD), jnp.bfloat16),
             pltpu.VMEM((heads, tok_rows, HEAD), jnp.bfloat16),
@@ -366,7 +436,7 @@
         compiler_params=pltpu.CompilerParams(
             collective_id=0, has_side_effects=True, vmem_limit_bytes=60 * 1024 * 1024
         ),
-    )(lens, queries, keys, values)
+    )(doc_lengths, queries, keys, values)
 
 
 def solution(mesh):

time: 80.2 us -> 77.2 us (0.963)
  the two profiles are of different devices: /device:TPU:29 before, /device:TPU:65 now
where the time goes in v3:
time: 77.2 us; the launch traced here: 77.1 us
  Pallas kernels  75.8 us (98%)
  local copies, waits for them, and re-layouts  1.27 us (2%)
    pallas_call x1, Pallas kernels, on_device(): pl.pallas_call(functools.partial(kernel, (cp_size, tp_size, half, groups,...  75.8 us

profile of v3, /device:TPU:65, one launch (start us, length us, event | category | flops | bytes accessed | tf_op | source)
XLA Modules:
  0.0 77.1 jit_solution(10361833778535386975)
XLA Ops:
  0.0 75.8 %shard_map.46 = bf16[192,5120]{1,0:T(8,128)(2,1)S(1)} custom-call(s32[64]{0:T(128)} %lens_ref.1, bf16[768,1280]{1,0:T(8,128)(2,1)} %q_hbm.1, bf16[768,256]{1,0:T(8,128)(2,1)} %k_hbm.1, bf16[768,256]{1,0:T(8,128)(2,1)} %v_hbm.1), custom_call_target="tpu_custom_call" | custom-call | tf_op jit(solution)/shard_map/pallas_call | solution.py:416
  75.8 1.3 %copy.6 = bf16[192,5120]{1,0:T(8,128)(2,1)} copy(bf16[192,5120]{1,0:T(8,128)(2,1)S(1)} %shard_map.46) | data formatting | bytes 3932160

commit v4 on v3

--- a/solution.py
+++ b/solution.py
@@ -14,8 +14,8 @@
 KEY_TILE = 256
 
 
-def kernel(sizes, lens_ref, q_hbm, k_hbm, v_hbm, out_hbm, kv, qbuf, bias, scores, outs,
-           load_sem, q_sem, kv_send, leap_send, kv_recv, out_send, out_recv, own_sem):
+def kernel(sizes, lens_ref, q_hbm, k_hbm, v_hbm, out_hbm, kv, passing, qbuf, bias, scores, outs,
+           load_sem, q_sem, kv_send, leap_send, kv_recv, pass_send, pass_recv, out_send, out_recv, own_sem):
     cp_size, tp_size, half, groups, kv_local = sizes
     heads = groups * kv_local
     chunk = 2 * half // tp_size
@@ -45,6 +45,21 @@
     mate = cp - 4 + 8 * below_gap
     near_first = near_gap & (near_way == 1 - below_gap)
 
+    wrap = middle - math.isqrt(middle)
+    odd = core == 1
+    upper_relay = chip - middle - wrap
+    lower_relay = middle - 1 - wrap - chip
+    relays_up = odd & (lower_relay >= 0) & (lower_relay <= 1)
+    relays_down = odd & (upper_relay >= 0) & (upper_relay <= 1)
+    is_relay = relays_up | relays_down
+    down = relays_down.astype(jnp.int32)
+    relay_slot = 2 - 2 * ((1 - down) * lower_relay + down * upper_relay)
+    relay_target = 2 * (middle - down) + 1
+    relay_source = cp + 2 * wrap * (1 - 2 * down)
+    detour_chip = odd & near_gap
+    is_target = odd & ((chip == middle - 1) | (chip == middle))
+    detour_via = cp - 2 * wrap * (2 * below_gap - 1)
+
     def beyond(direction):
         return (1 - direction) * above + direction * below
 
@@ -58,7 +73,13 @@
         return chip == middle - 1 + direction
 
     def leaps(direction):
-        return chip == middle - 2 + 3 * direction
+        return (chip == middle - 2 + 3 * direction) & (core == 0)
+
+    def detours(direction):
+        return odd & (stops(direction) | (chip == middle - 2 + 3 * direction))
+
+    def hops(direction):
+        return jnp.logical_not(odd & stops(direction))
 
     def load(direction, g, part):
         src = (k_hbm, v_hbm)[part]
@@ -90,6 +111,26 @@
             send_sem=leap_send.at[direction, g, part],
             recv_sem=kv_recv.at[direction, g, part, 0],
             device_id=(cp + 4 - 8 * direction, tp),
+            device_id_type=MESH,
+        )
+
+    def detour(g, part):
+        return pltpu.make_async_remote_copy(
+            src_ref=slot(1 - below_gap, g, part, 4),
+            dst_ref=passing.at[g, part],
+            send_sem=leap_send.at[1 - below_gap, g, part],
+            recv_sem=pass_recv.at[g, part],
+            device_id=(detour_via, tp),
+            device_id_type=MESH,
+        )
+
+    def forward(g, part):
+        return pltpu.make_async_remote_copy(
+            src_ref=passing.at[g, part],
+            dst_ref=slot(down, g, part, relay_slot),
+            send_sem=pass_send.at[g, part],
+            recv_sem=kv_recv.at[down, g, part, relay_slot],
+            device_id=(relay_target, tp),
             device_id_type=MESH,
         )
 
@@ -115,7 +156,14 @@
 
     def offer(direction, g, part):
         load(direction, g, part).wait()
-        hop(direction, g, part, 0).start()
+
+        @pl.when(hops(direction))
+        def _():
+            hop(direction, g, part, 0).start()
+
+        @pl.when(detours(direction))
+        def _():
+            detour(g, part).start()
 
         @pl.when(leaps(direction))
         def _():
@@ -194,6 +242,23 @@
     def _():
         pl.semaphore_signal(barrier, inc=1, device_id=(mate, tp), device_id_type=MESH)
 
+    @pl.when(detour_chip)
+    def _():
+        pl.semaphore_signal(barrier, inc=1, device_id=(detour_via, tp), device_id_type=MESH)
+
+    @pl.when(is_relay)
+    def _():
+        for device in (relay_source, relay_target):
+            pl.semaphore_signal(barrier, inc=1, device_id=(device, tp), device_id_type=MESH)
+
+    @pl.when(is_target)
+    def _():
+        for step in range(2):
+            low_relay = middle - 1 - wrap - step
+            high_relay = middle + wrap + step
+            device = 2 * (below_gap * high_relay + (1 - below_gap) * low_relay) + 1
+            pl.semaphore_signal(barrier, inc=1, device_id=(device, tp), device_id_type=MESH)
+
     for direction in (far_way, near_way):
         for g in range(kv_local):
             for part in range(2):
@@ -201,16 +266,23 @@
     for h in range(heads):
         load_q(h).start()
 
-    pl.semaphore_wait(barrier, 6 + near_gap.astype(jnp.int32))
+    greetings = (
+        6 + near_gap.astype(jnp.int32) + detour_chip.astype(jnp.int32)
+        + 2 * is_relay.astype(jnp.int32) + 2 * is_target.astype(jnp.int32)
+    )
+    pl.semaphore_wait(barrier, greetings)
 
     offer(far_way, 0, 0)
     offer(far_way, 0, 1)
 
-    @pl.when(jnp.logical_not(near_gap))
-    def _():
-        offer(near_way, 0, 0)
-        offer(near_way, 0, 1)
-
+    offer(near_way, 0, 0)
+    offer(near_way, 0, 1)
+
+    @pl.when(near_gap)
+    def _():
+        for way in (far_way, near_way):
+            offer(way, 1, 0)
+            offer(way, 1, 1)
 
     row = lax.broadcasted_iota(jnp.int32, (HEAD, HEAD), 0)
     col = lax.broadcasted_iota(jnp.int32, (HEAD, HEAD), 1)
@@ -240,13 +312,6 @@
     for h in range(heads):
         load_q(h).wait()
 
-    @pl.when(near_gap)
-    def _():
-        hop(far_way, 0, 1, 0).wait_send()
-        for way, g in ((near_way, 0), (far_way, 1), (near_way, 1)):
-            offer(way, g, 0)
-            offer(way, g, 1)
-
     @pl.when(near_first)
     def _():
         for g in range(kv_local):
@@ -261,6 +326,20 @@
         for way in (far_way, near_way):
             offer(way, 1, 0)
             offer(way, 1, 1)
+
+    @pl.when(is_relay)
+    def _():
+        for g in range(kv_local):
+            for part in range(2):
+                pltpu.make_async_remote_copy(
+                    src_ref=passing.at[g, part],
+                    dst_ref=passing.at[g, part],
+                    send_sem=pass_send.at[g, part],
+                    recv_sem=pass_recv.at[g, part],
+                    device_id=(relay_source, tp),
+                    device_id_type=MESH,
+                ).wait_recv()
+                forward(g, part).start()
 
     @pl.when(is_end)
     def _():
@@ -374,14 +453,14 @@
     for g in range(kv_local):
         for part in range(2):
             for way in (far_way, near_way):
-                if g == 0 and part == 1 and way is far_way:
-
-                    @pl.when(jnp.logical_not(near_gap))
-                    def _():
-                        hop(way, g, part, 0).wait_send()
-
-                else:
+                @pl.when(hops(way))
+                def _():
                     hop(way, g, part, 0).wait_send()
+
+                @pl.when(detours(way))
+                def _():
+                    detour(g, part).wait_send()
+
                 across(way, g, part, 0).wait_send()
                 across(way, g, part, 1).wait_send()
 
@@ -392,6 +471,12 @@
                 @pl.when(leaps(way))
                 def _():
                     leap(way, g, part).wait_send()
+
+    @pl.when(is_relay)
+    def _():
+        for g in range(kv_local):
+            for part in range(2):
+                forward(g, part).wait_send()
 
     def drain(i, carry):
         turn, h = i // heads, i % heads
@@ -420,6 +505,7 @@
         out_specs=pl.BlockSpec(memory_space=pltpu.VMEM),
         scratch_shapes=[
             pltpu.VMEM((2, kv_local, 2, 5 * half, HEAD), jnp.bfloat16),
+            pltpu.VMEM((kv_local, 2, half, HEAD), jnp.bfloat16),
             pltpu.VMEM((heads, tok_rows, HEAD), jnp.bfloat16),
             pltpu.VMEM((4, chunk, window), jnp.float32),
             pltpu.VMEM((2, chunk, window), jnp.float32),
@@ -429,6 +515,8 @@
             pltpu.SemaphoreType.DMA((2, kv_local, 2, 4)),
             pltpu.SemaphoreType.DMA((2, kv_local, 2)),
             pltpu.SemaphoreType.DMA((2, kv_local, 2, 4)),
+            pltpu.SemaphoreType.DMA((kv_local, 2)),
+            pltpu.SemaphoreType.DMA((kv_local, 2)),
             pltpu.SemaphoreType.DMA((3, heads)),
             pltpu.SemaphoreType.DMA((3, heads)),
             pltpu.SemaphoreType.DMA((heads,)),

time: 77.2 us -> 71.4 us (0.925)
  the two profiles are of different devices: /device:TPU:65 before, /device:TPU:93 now
where the time goes in v4:
time: 71.4 us; the launch traced here: 70.8 us
  Pallas kernels  69.5 us (97%)
  local copies, waits for them, and re-layouts  1.27 us (2%)
    pallas_call x1, Pallas kernels, on_device(): pl.pallas_call(functools.partial(kernel, (cp_size, tp_size, half, groups,...  69.5 us

profile of v4, /device:TPU:93, one launch (start us, length us, event | category | flops | bytes accessed | tf_op | source)
XLA Modules:
  0.0 70.8 jit_solution(12290680129376303204)
XLA Ops:
  0.0 69.5 %shard_map.46 = bf16[192,5120]{1,0:T(8,128)(2,1)S(1)} custom-call(s32[64]{0:T(128)} %lens_ref.1, bf16[768,1280]{1,0:T(8,128)(2,1)} %q_hbm.1, bf16[768,256]{1,0:T(8,128)(2,1)} %k_hbm.1, bf16[768,256]{1,0:T(8,128)(2,1)} %v_hbm.1), custom_call_target="tpu_custom_call" | custom-call | tf_op jit(solution)/shard_map/pallas_call | solution.py:501
  69.5 1.3 %copy.6 = bf16[192,5120]{1,0:T(8,128)(2,1)} copy(bf16[192,5120]{1,0:T(8,128)(2,1)S(1)} %shard_map.46) | data formatting | bytes 3932160

commit v5 on v4

--- a/solution.py
+++ b/solution.py
@@ -45,20 +45,20 @@
     mate = cp - 4 + 8 * below_gap
     near_first = near_gap & (near_way == 1 - below_gap)
 
-    wrap = middle - math.isqrt(middle)
+    along_x = math.isqrt(middle) - 1
+    along_y = middle - math.isqrt(middle)
     odd = core == 1
-    upper_relay = chip - middle - wrap
-    lower_relay = middle - 1 - wrap - chip
-    relays_up = odd & (lower_relay >= 0) & (lower_relay <= 1)
-    relays_down = odd & (upper_relay >= 0) & (upper_relay <= 1)
+    relays_up = odd & ((chip == middle - 1 - along_x) | (chip == middle - 2 - along_y))
+    relays_down = odd & ((chip == middle + along_x) | (chip == middle + 1 + along_y))
     is_relay = relays_up | relays_down
     down = relays_down.astype(jnp.int32)
-    relay_slot = 2 - 2 * ((1 - down) * lower_relay + down * upper_relay)
+    for_slot_2 = ((chip == middle - 1 - along_x) | (chip == middle + along_x)).astype(jnp.int32)
+    relay_slot = 2 * for_slot_2
     relay_target = 2 * (middle - down) + 1
-    relay_source = cp + 2 * wrap * (1 - 2 * down)
-    detour_chip = odd & near_gap
-    is_target = odd & ((chip == middle - 1) | (chip == middle))
-    detour_via = cp - 2 * wrap * (2 * below_gap - 1)
+    relay_source = cp + 2 * (for_slot_2 * along_x + (1 - for_slot_2) * along_y) * (1 - 2 * down)
+    is_middle = (chip == middle - 1) | (chip == middle)
+    at_middle = is_middle.astype(jnp.int32)
+    detour_via = cp - 2 * (at_middle * along_x + (1 - at_middle) * along_y) * (2 * below_gap - 1)
 
     def beyond(direction):
         return (1 - direction) * above + direction * below
@@ -235,28 +235,28 @@
     for turn in range(3):
         high, low = peer_of(turn)
         pl.semaphore_signal(barrier, inc=1, device_id=(cp, 2 * high + low), device_id_type=MESH)
-    for device in (above, below, partner):
-        pl.semaphore_signal(barrier, inc=1, device_id=(device, tp), device_id_type=MESH)
-
-    @pl.when(near_gap)
+    pl.semaphore_signal(barrier, inc=1, device_id=(partner, tp), device_id_type=MESH)
+
+    @pl.when(jnp.logical_not(odd & (chip == middle - 1)))
+    def _():
+        pl.semaphore_signal(barrier, inc=1, device_id=(above, tp), device_id_type=MESH)
+
+    @pl.when(jnp.logical_not(odd & (chip == middle)))
+    def _():
+        pl.semaphore_signal(barrier, inc=1, device_id=(below, tp), device_id_type=MESH)
+
+    @pl.when(is_middle & (core == 0))
     def _():
         pl.semaphore_signal(barrier, inc=1, device_id=(mate, tp), device_id_type=MESH)
 
-    @pl.when(detour_chip)
-    def _():
-        pl.semaphore_signal(barrier, inc=1, device_id=(detour_via, tp), device_id_type=MESH)
-
     @pl.when(is_relay)
     def _():
-        for device in (relay_source, relay_target):
-            pl.semaphore_signal(barrier, inc=1, device_id=(device, tp), device_id_type=MESH)
-
-    @pl.when(is_target)
-    def _():
-        for step in range(2):
-            low_relay = middle - 1 - wrap - step
-            high_relay = middle + wrap + step
-            device = 2 * (below_gap * high_relay + (1 - below_gap) * low_relay) + 1
+        pl.semaphore_signal(barrier, inc=1, device_id=(relay_source, tp), device_id_type=MESH)
+
+    @pl.when(is_middle & odd)
+    def _():
+        for step in (along_x, 1 + along_y):
+            device = 2 * (below_gap * (middle + step) + (1 - below_gap) * (middle - 1 - step)) + 1
             pl.semaphore_signal(barrier, inc=1, device_id=(device, tp), device_id_type=MESH)
 
     for direction in (far_way, near_way):
@@ -267,22 +267,17 @@
         load_q(h).start()
 
     greetings = (
-        6 + near_gap.astype(jnp.int32) + detour_chip.astype(jnp.int32)
-        + 2 * is_relay.astype(jnp.int32) + 2 * is_target.astype(jnp.int32)
+        6 + (near_gap & jnp.logical_not(is_middle)).astype(jnp.int32) + is_relay.astype(jnp.int32)
     )
     pl.semaphore_wait(barrier, greetings)
 
     offer(far_way, 0, 0)
     offer(far_way, 0, 1)
 
-    offer(near_way, 0, 0)
-    offer(near_way, 0, 1)
-
-    @pl.when(near_gap)
-    def _():
-        for way in (far_way, near_way):
-            offer(way, 1, 0)
-            offer(way, 1, 1)
+    @pl.when(jnp.logical_not(near_gap))
+    def _():
+        offer(near_way, 0, 0)
+        offer(near_way, 0, 1)
 
     row = lax.broadcasted_iota(jnp.int32, (HEAD, HEAD), 0)
     col = lax.broadcasted_iota(jnp.int32, (HEAD, HEAD), 1)
@@ -312,24 +307,15 @@
     for h in range(heads):
         load_q(h).wait()
 
-    @pl.when(near_first)
-    def _():
-        for g in range(kv_local):
-            relay(near_way, g, 0)
-            relay(near_way, g, 1)
-
-    relay(far_way, 0, 0)
-    relay(far_way, 0, 1)
-
-    @pl.when(jnp.logical_not(near_gap))
-    def _():
-        for way in (far_way, near_way):
-            offer(way, 1, 0)
-            offer(way, 1, 1)
-
-    @pl.when(is_relay)
-    def _():
-        for g in range(kv_local):
+    @pl.when(near_gap)
+    def _():
+        for way, g in ((far_way, 1), (near_way, 0), (near_way, 1)):
+            offer(way, g, 0)
+            offer(way, g, 1)
+
+    def pass_on(g):
+        @pl.when(is_relay)
+        def _():
             for part in range(2):
                 pltpu.make_async_remote_copy(
                     src_ref=passing.at[g, part],
@@ -341,6 +327,23 @@
                 ).wait_recv()
                 forward(g, part).start()
 
+    pass_on(0)
+    relay(far_way, 0, 0)
+    relay(far_way, 0, 1)
+
+    @pl.when(near_first)
+    def _():
+        relay(near_way, 0, 0)
+        relay(near_way, 0, 1)
+
+    @pl.when(jnp.logical_not(near_gap))
+    def _():
+        for way in (far_way, near_way):
+            offer(way, 1, 0)
+            offer(way, 1, 1)
+
+    pass_on(1)
+
     @pl.when(is_end)
     def _():
         relay(near_way, 0, 0)
@@ -372,6 +375,11 @@
         def _():
             relay(far_way, 1, 0)
             relay(far_way, 1, 1)
+
+            @pl.when(near_first)
+            def _():
+                relay(near_way, 1, 0)
+                relay(near_way, 1, 1)
 
         @pl.when(u == 2)
         def _():

time: 71.4 us -> 69.6 us (0.975)
  Pallas kernels: 69.5 us -> 68.2 us
    pallas_call x1, Pallas kernels: 69.5 us -> 68.2 us  [on_device(): pl.pallas_call(functools.partial(kernel, (cp_size, tp_size, half, groups,...]
where the time goes in v5:
time: 69.6 us; the launch traced here: 69.5 us
  Pallas kernels  68.2 us (98%)
  local copies, waits for them, and re-layouts  1.27 us (2%)
    pallas_call x1, Pallas kernels, on_device(): pl.pallas_call(functools.partial(kernel, (cp_size, tp_size, half, groups,...  68.2 us

profile of v5, /device:TPU:93, one launch (start us, length us, event | category | flops | bytes accessed | tf_op | source)
XLA Modules:
  0.0 69.5 jit_solution(4576328020135570097)
XLA Ops:
  0.0 68.2 %shard_map.46 = bf16[192,5120]{1,0:T(8,128)(2,1)S(1)} custom-call(s32[64]{0:T(128)} %lens_ref.1, bf16[768,1280]{1,0:T(8,128)(2,1)} %q_hbm.1, bf16[768,256]{1,0:T(8,128)(2,1)} %k_hbm.1, bf16[768,256]{1,0:T(8,128)(2,1)} %v_hbm.1), custom_call_target="tpu_custom_call" | custom-call | tf_op jit(solution)/shard_map/pallas_call | solution.py:509
  68.3 1.3 %copy.6 = bf16[192,5120]{1,0:T(8,128)(2,1)} copy(bf16[192,5120]{1,0:T(8,128)(2,1)S(1)} %shard_map.46) | data formatting | bytes 3932160

commit v6 on v5

--- a/solution.py
+++ b/solution.py
@@ -14,8 +14,9 @@
 KEY_TILE = 256
 
 
-def kernel(sizes, lens_ref, q_hbm, k_hbm, v_hbm, out_hbm, kv, passing, qbuf, bias, scores, outs,
-           load_sem, q_sem, kv_send, leap_send, kv_recv, pass_send, pass_recv, out_send, out_recv, own_sem):
+def kernel(sizes, lens_hbm, q_hbm, k_hbm, v_hbm, out_hbm, kv, passing, qbuf, bias, scores, outs,
+           load_sem, q_sem, kv_send, leap_send, kv_recv, pass_send, pass_recv, out_send, out_recv, own_sem,
+           lens_ref, lens_sem):
     cp_size, tp_size, half, groups, kv_local = sizes
     heads = groups * kv_local
     chunk = 2 * half // tp_size
@@ -263,6 +264,8 @@
         for g in range(kv_local):
             for part in range(2):
                 load(direction, g, part).start()
+    load_lens = pltpu.make_async_copy(lens_hbm, lens_ref, lens_sem)
+    load_lens.start()
     for h in range(heads):
         load_q(h).start()
 
@@ -282,6 +285,7 @@
     row = lax.broadcasted_iota(jnp.int32, (HEAD, HEAD), 0)
     col = lax.broadcasted_iota(jnp.int32, (HEAD, HEAD), 1)
     upper = (row <= col).astype(jnp.float32)
+    load_lens.wait()
     docs = lens_ref.shape[-1]
     lens = jnp.concatenate(
         [lens_ref[...].reshape(1, docs).astype(jnp.float32), jnp.zeros((1, HEAD - docs), jnp.float32)], axis=1
@@ -509,7 +513,7 @@
     return pl.pallas_call(
         functools.partial(kernel, (cp_size, tp_size, half, groups, kv_local)),
         out_shape=pltpu.VMEM((chunk, q_cols * tp_size), jnp.bfloat16),
-        in_specs=[pl.BlockSpec(memory_space=pltpu.VMEM), hbm, hbm, hbm],
+        in_specs=[hbm, hbm, hbm, hbm],
         out_specs=pl.BlockSpec(memory_space=pltpu.VMEM),
         scratch_shapes=[
             pltpu.VMEM((2, kv_local, 2, 5 * half, HEAD), jnp.bfloat16),
@@ -528,6 +532,8 @@
             pltpu.SemaphoreType.DMA((3, heads)),
             pltpu.SemaphoreType.DMA((3, heads)),
             pltpu.SemaphoreType.DMA((heads,)),
+            pltpu.VMEM(doc_lengths.shape, jnp.int32),
+            pltpu.SemaphoreType.DMA,
         ],
         compiler_params=pltpu.CompilerParams(
             collective_id=0, has_side_effects=True, vmem_limit_bytes=60 * 1024 * 1024

time: 69.6 us -> 69 us (level)
  no operation moved by 1% of the time
where the time goes in v6:
time: 69 us; the launch traced here: 68.9 us
  Pallas kernels  67.6 us (98%)
  local copies, waits for them, and re-layouts  1.27 us (2%)
    pallas_call x1, Pallas kernels, on_device(): pl.pallas_call(functools.partial(kernel, (cp_size, tp_size, half, groups,...  67.6 us

profile of v6, /device:TPU:93, one launch (start us, length us, event | category | flops | bytes accessed | tf_op | source)
XLA Modules:
  0.0 68.9 jit_solution(6995019822267720421)
XLA Ops:
  0.0 67.6 %shard_map.46 = bf16[192,5120]{1,0:T(8,128)(2,1)S(1)} custom-call(s32[64]{0:T(128)} %lens_hbm.1, bf16[768,1280]{1,0:T(8,128)(2,1)} %q_hbm.1, bf16[768,256]{1,0:T(8,128)(2,1)} %k_hbm.1, bf16[768,256]{1,0:T(8,128)(2,1)} %v_hbm.1), custom_call_target="tpu_custom_call" | custom-call | tf_op jit(solution)/shard_map/pallas_call | solution.py:513
  67.6 1.3 %copy.6 = bf16[192,5120]{1,0:T(8,128)(2,1)} copy(bf16[192,5120]{1,0:T(8,128)(2,1)S(1)} %shard_map.46) | data formatting | bytes 3932160
